TPU v7x, 128 devices: a whole 4x4x4 slice. The times are simulated.
128 devices in a mesh: gx: 4 (over y), gy: 8 (over z, x_hi), gz: 4 (over x_lo, core).
Axes of the slice: x: 4 (x_hi: 2, x_lo: 2; x = x_hi * 2 + x_lo), y: 4, z: 4, core: 2. Of those that a mesh axis runs over, the one named last changes fastest.
Arguments:
- right_side: float32 [64, 1024, 1024], P('gz', 'gx', 'gy'), may hold values from -8 to 8
- diagonal: float32 [64, 1024, 1024], P('gz', 'gx', 'gy'), may hold values from 0.02 to 1
- regime: int32 [1024, 1024], P('gx', 'gy'), may hold values from 0 to 7
- inverses: float32 [8, 64, 64], replicated, as said below
Outputs:
- solution: float32 [64, 1024, 1024], P('gz', 'gx', 'gy')
- residual: float32 [64, 1024, 1024], P('gz', 'gx', 'gy')
Inputs may be any that keep to these rules, and one draw needn't show every extreme that they name: `inverses`: each block is symmetric positive definite.
All inputs are finite; a program needn't handle non-finite values.
Results may differ from a plain program's by a relative error of at most 0.00025.
Values sent between devices are 32-bit elements; how exact they have to be, the bound alone decides.
A program may use at most 128 MiB of HBM per device.

v0:
```python
import jax
import jax.numpy as jnp
from jax import lax
from jax.sharding import Mesh
from jax.sharding import PartitionSpec as P

NREG = 8
ITERS = 3
GX_GZ = ("gx", "gz_0", "gz_1")
GY = ("gy_0", "gy_1")
GZ = ("gz_0", "gz_1")
GX_GY_GZ = ("gx", "gy_0", "gy_1", "gz_0", "gz_1")


def extended(cells, sides, width):
    for axis, dim in sides:
        count = lax.axis_size(axis)
        ends = count - 1
        head = lax.slice_in_dim(cells, 0, width, axis=dim)
        tail = lax.slice_in_dim(cells, cells.shape[dim] - width, cells.shape[dim], axis=dim)
        cells = jnp.concatenate(
            [
                lax.ppermute(tail, axis, [(i, (i + 1) % count) for i in range(ends)]),
                cells,
                lax.ppermute(head, axis, [((i + 1) % count, i) for i in range(ends)]),
            ],
            axis=dim,
        )
    return cells


def over_axes(x, axes):
    for axis in axes:
        x = lax.psum(x, axis)
    return x


def sent_together(arrays, axis, split_dim, concat_dim, along):
    ends, at = ([], 0)
    for a in arrays[:-1]:
        at += a.shape[along]
        ends.append(at)
    both = jnp.concatenate(arrays, axis=along)
    return tuple(
        jnp.split(
            lax.all_to_all(both, axis, split_axis=split_dim, concat_axis=concat_dim, tiled=True),
            ends,
            axis=along,
        )
    )


def stencil(padded, grid_field, diagonal):
    beside = padded[2:, 1:-1, 1:-1] + padded[:-2, 1:-1, 1:-1]
    beside = beside + padded[1:-1, 2:, 1:-1] + padded[1:-1, :-2, 1:-1]
    beside = beside + padded[1:-1, 1:-1, 2:] + padded[1:-1, 1:-1, :-2]
    return (6.0 + diagonal) * grid_field - beside


def operate(grid_field, diagonal):
    flat_pad = extended(grid_field, ((GX_GZ, 1), (GY, 2)), 1)
    padded = jnp.pad(flat_pad, ((1, 1), (0, 0), (0, 0)))
    return stencil(padded, grid_field, diagonal)


def apply_blocks(matrices, flattened, chosen):
    result = jnp.zeros((matrices.shape[1], flattened.shape[1]), jnp.float32)
    for member in range(NREG):
        product = jnp.dot(matrices[member], flattened, precision=lax.Precision.HIGHEST)
        result = result + jnp.where(chosen[None, :] == member, product, jnp.zeros_like(product))
    return result


def precondition(grid_field, regime, inverses):
    layers = grid_field.shape[0]
    share_rows = grid_field.shape[1]
    offset = lax.axis_index(GZ) * share_rows
    chosen = lax.dynamic_slice_in_dim(regime, offset, share_rows, 0).reshape(-1)
    result = apply_blocks(inverses, grid_field.reshape(layers, -1), chosen)
    return result.reshape(grid_field.shape)


def paired(residual, precond, image):
    return (
        over_axes(jnp.sum(residual * precond), GX_GY_GZ),
        over_axes(jnp.sum(image * precond), GX_GY_GZ),
    )


def per_device(right_side, diagonal, regime, inverses):
    right_side, diagonal = (
        lax.all_to_all(right_side, GZ, split_axis=1, concat_axis=0, tiled=True),
        lax.all_to_all(diagonal, GZ, split_axis=1, concat_axis=0, tiled=True),
    )
    solution = jnp.zeros_like(right_side)
    residual = right_side
    precond = precondition(residual, regime, inverses)
    image = operate(precond, diagonal)
    inner_rz, inner_wz = paired(residual, precond, image)
    step_len = inner_rz / inner_wz
    search = precond
    along = image
    for iteration in range(ITERS):
        solution = solution + step_len * search
        residual = residual - step_len * along
        if iteration + 1 < ITERS:
            precond = precondition(residual, regime, inverses)
            image = operate(precond, diagonal)
            rz_next, inner_wz = paired(residual, precond, image)
            scaling = rz_next / inner_rz
            step_len = rz_next / (inner_wz - scaling * rz_next / step_len)
            search = precond + scaling * search
            along = image + scaling * along
            inner_rz = rz_next
    solution, residual = sent_together((solution, residual), GZ, 0, 1, 2)
    return (solution, residual)


def solution(mesh):
    split = Mesh(
        mesh.devices.reshape(mesh.shape["gx"], 4, 2, 2, 2), ("gx", "gy_0", "gy_1", "gz_0", "gz_1")
    )
    in_specs = (P(GZ, "gx", GY), P(GZ, "gx", GY), P("gx", GY), P())
    out_specs = (P(GZ, "gx", GY), P(GZ, "gx", GY))
    return jax.shard_map(
        per_device, mesh=split, in_specs=in_specs, out_specs=out_specs, check_vma=False
    )
```

profile of v0, /device:TPU:1, one launch (start us, length us, event | category | flops | bytes accessed | tf_op | source)
XLA Modules:
  0.0 442.0 jit_solution(1391907388788264232)
XLA Ops:
  0.6 4.1 copy.125
  4.8 5.0 %all-to-all-start = ((f32[16,256,128]{2,0,1:T(8,128)}), f32[16,256,128]{2,0,1:T(8,128)S(1)}, u32[]{:S(2)}, u32[]{:S(2)}) async-start(f32[16,256,128]{2,0,1:T(8,128)} %copy.125), calls=%async_computation | async-start | bytes 4194304 | tf_op jit(solution)/shard_map/all_to_all | solution.py:92
  9.7 4.1 copy.127
  14.6 19.8 %all-to-all-done = f32[16,256,128]{2,0,1:T(8,128)S(1)} async-done(((f32[16,256,128]{2,0,1:T(8,128)}), f32[16,256,128]{2,0,1:T(8,128)S(1)}, u32[]{:S(2)}, u32[]{:S(2)}) %all-to-all-start) | async-done | bytes 2097184 | tf_op jit(solution)/shard_map/all_to_all | solution.py:92
  34.4 5.9 %all-to-all-start.1 = ((f32[16,256,128]{2,0,1:T(8,128)}), f32[16,256,128]{2,0,1:T(8,128)}, u32[]{:S(2)}, u32[]{:S(2)}) async-start(f32[16,256,128]{2,0,1:T(8,128)} %copy.127), calls=%async_computation.1 | async-start | bytes 4194304 | tf_op jit(solution)/shard_map/all_to_all | solution.py:93
  41.3 3.1 convolution_select_fusion.23
  44.3 3.2 fusion.20
  47.5 3.2 fusion.19
  50.7 3.4 fusion.18
  54.1 3.2 fusion.17
  57.3 3.2 fusion.16
  60.5 3.2 fusion.15
  63.7 3.4 fusion.62
  69.6 3.6 collective-permute-start
  73.2 3.0 broadcast_add_fusion
  76.6 2.8 fusion.149
  84.3 4.8 %collective-permute-start.2 = (f32[64,66,1]{1,0,2:T(8,128)S(1)}, f32[64,66,1]{1,0,2:T(8,128)S(1)}, u32[]{:S(2)}, u32[]{:S(2)}) collective-permute-start(f32[64,66,1]{1,0,2:T(8,128)S(1)} %copy.133), channel_id=1, source_target_pairs={{0,4},{4,8},{8,12},{12,16},{16,20},{20,24},{24,28},{1,5},{5,9},{9,... | collective-permute-start | bytes 50696 | tf_op jit(solution)/shard_map/ppermute | solution.py:23
  90.4 3.1 fusion.38
  100.0 5.4 %select_maximum_fusion.8 = f32[66,66,130]{2,1,0:T(8,128)S(1)} fusion(f32[64,66,1]{2,1,0:T(8,128)} %copy.136, f32[64,66,1]{2,1,0:T(8,128)} %copy.135, f32[64,1,128]{2,1,0:T(1,128)S(1)} %bitcast.246, f32[64,64,128]{2,1,0:T(8,128)S(1)} %bitcast.230, f32[64,1,128]{2,1,0:T(1,128)S(1)} %bitcast.249), kind=kLoop, calls=%fused_computation.55 | loop fusion | flops 6795360 | bytes 4461600 | tf_op jit(solution)/shard_map/concatenate | solution.py:21
  105.5 5.7 %multiply_reduce_fusion.4 = (f32[]{:T(128)}, f32[64,64,128]{2,1,0:T(8,128)}) fusion(f32[8,8,64,128]{3,2,1,0:T(8,128)S(1)} %copy.167, f32[64,1,128]{2,1,0:T(1,128)S(1)} %bitcast.247, f32[64,64,128]{2,1,0:T(8,128)S(1)} %bitcast.231, f32[64,1,128]{2,1,0:T(1,128)S(1)} %bitcast.250, f32[64,66,1]{2,1,0:T(8,128)S(1)} %copy-done.15, ...), kind=kLoop, calls=%fused_computation.144 | loop fusion | flops 8912895 | bytes 12682244 | tf_op jit(solution)/shard_map/reduce_sum | solution.py:86
  111.2 9.4 %all-reduce.8 = (f32[]{:T(128)}, f32[]{:T(128)}) all-reduce(f32[]{:T(128)} %fusion.38, f32[]{:T(128)} %get-tuple-element.38), channel_id=1, replica_groups=mesh['gx'=4,'gy_0'=4,'gy_1'=2,'gz_0'=2,'gz_1'=2] {'gx'}, use_global_device_ids=true, to_apply=%region_1.2 | all-reduce | flops 2 | bytes 16 | tf_op jit(solution)/shard_map/psum | solution.py:34
  120.6 12.2 %all-reduce.5 = (f32[]{:T(128)}, f32[]{:T(128)}) all-reduce(f32[]{:T(128)} %get-tuple-element.16, f32[]{:T(128)} %get-tuple-element.17), channel_id=1, replica_groups=mesh['gx'=4,'gy_0'=4,'gy_1'=2,'gz_0'=2,'gz_1'=2] {'gy_0'}, use_global_device_ids=true, to_apply=%region_2.3 | all-reduce | flops 2 | bytes 16 | tf_op jit(solution)/shard_map/psum | solution.py:34
  132.7 6.0 %all-reduce.17 = (f32[]{:T(128)}, f32[]{:T(128)}) all-reduce(f32[]{:T(128)} %get-tuple-element.10, f32[]{:T(128)} %get-tuple-element.11), channel_id=1, replica_groups=mesh['gx'=4,'gy_0'=4,'gy_1'=2,'gz_0'=2,'gz_1'=2] {'gy_1'}, use_global_device_ids=true, to_apply=%region_3.4 | all-reduce | flops 2 | bytes 16 | tf_op jit(solution)/shard_map/psum | solution.py:34
  138.7 4.5 %all-reduce.14 = (f32[]{:T(128)}, f32[]{:T(128)}) all-reduce(f32[]{:T(128)} %get-tuple-element.34, f32[]{:T(128)} %get-tuple-element.35), channel_id=1, replica_groups=mesh['gx'=4,'gy_0'=4,'gy_1'=2,'gz_0'=2,'gz_1'=2] {'gz_0'}, use_global_device_ids=true, to_apply=%region_4.5 | all-reduce | flops 2 | bytes 16 | tf_op jit(solution)/shard_map/psum | solution.py:34
  143.2 11.4 %all-reduce.11 = (f32[]{:T(128)}, f32[]{:T(128)}) all-reduce(f32[]{:T(128)} %get-tuple-element.28, f32[]{:T(128)} %get-tuple-element.29), channel_id=1, replica_groups=mesh['gx'=4,'gy_0'=4,'gy_1'=2,'gz_0'=2,'gz_1'=2] {'gz_1'}, use_global_device_ids=true, to_apply=%region_5.6 | all-reduce | flops 2 | bytes 16 | tf_op jit(solution)/shard_map/psum | solution.py:34
  158.5 3.3 convolution_select_fusion.15
  161.8 3.4 fusion.13
  165.2 3.4 fusion.12
  168.6 3.6 fusion.11
  172.2 3.4 fusion.10
  175.7 3.4 fusion.9
  179.1 3.4 fusion.8
  182.5 3.6 fusion.65
  188.9 3.3 collective-permute-start.4
  193.6 2.8 fusion.148
  202.6 5.5 %collective-permute-start.6 = (f32[64,66,1]{1,0,2:T(8,128)S(1)}, f32[64,66,1]{1,0,2:T(8,128)S(1)}, u32[]{:S(2)}, u32[]{:S(2)}) collective-permute-start(f32[64,66,1]{1,0,2:T(8,128)S(1)} %copy.145), channel_id=1, source_target_pairs={{0,4},{4,8},{8,12},{12,16},{16,20},{20,24},{24,28},{1,5},{5,9},{9,... | collective-permute-start | bytes 50696 | tf_op jit(solution)/shard_map/ppermute | solution.py:23
  212.7 6.2 %select_maximum_fusion.4 = f32[66,66,130]{2,1,0:T(8,128)S(1)} fusion(f32[64,66,1]{2,1,0:T(8,128)} %copy.148, f32[64,66,1]{2,1,0:T(8,128)} %copy.147, f32[64,1,128]{2,1,0:T(1,128)S(1)} %bitcast.255, f32[64,64,128]{2,1,0:T(8,128)} %bitcast.234, f32[64,1,128]{2,1,0:T(1,128)S(1)} %bitcast.261), kind=kLoop, calls=%fused_computation.51 | loop fusion | flops 6795360 | bytes 4461600 | tf_op jit(solution)/shard_map/concatenate | solution.py:21
  218.9 6.0 %multiply_reduce_fusion.2 = (f32[]{:T(128)}, f32[]{:T(128)}, f32[64,64,128]{2,1,0:T(8,128)}) fusion(f32[8,8,64,128]{3,2,1,0:T(8,128)S(1)} %copy-done.4, f32[64,64,128]{2,1,0:T(8,128)S(1)} %bitcast_subtract_fusion, f32[64,1,128]{2,1,0:T(1,128)S(1)} %bitcast.256, f32[64,64,128]{2,1,0:T(8,128)S(1)} %bitcast.235, f32[64,1,128]{2,1,0:T(1,128)S(1)} %bitcast.262, ...), kind=kLoop, calls=%fused_computation.142 | loop fusion | flops 9961470 | bytes 14779400 | tf_op jit(solution)/shard_map/reduce_sum | solution.py:86
  224.9 7.0 %all-reduce.7 = (f32[]{:T(128)}, f32[]{:T(128)}) all-reduce(f32[]{:T(128)} %get-tuple-element.5, f32[]{:T(128)} %get-tuple-element.4), channel_id=1, replica_groups=mesh['gx'=4,'gy_0'=4,'gy_1'=2,'gz_0'=2,'gz_1'=2] {'gx'}, use_global_device_ids=true, to_apply=%region_13.14 | all-reduce | flops 2 | bytes 16 | tf_op jit(solution)/shard_map/psum | solution.py:34
  231.9 9.4 %all-reduce.4 = (f32[]{:T(128)}, f32[]{:T(128)}) all-reduce(f32[]{:T(128)} %get-tuple-element.14, f32[]{:T(128)} %get-tuple-element.15), channel_id=1, replica_groups=mesh['gx'=4,'gy_0'=4,'gy_1'=2,'gz_0'=2,'gz_1'=2] {'gy_0'}, use_global_device_ids=true, to_apply=%region_14.15 | all-reduce | flops 2 | bytes 16 | tf_op jit(solution)/shard_map/psum | solution.py:34
  241.3 6.0 %all-reduce.16 = (f32[]{:T(128)}, f32[]{:T(128)}) all-reduce(f32[]{:T(128)} %get-tuple-element.8, f32[]{:T(128)} %get-tuple-element.9), channel_id=1, replica_groups=mesh['gx'=4,'gy_0'=4,'gy_1'=2,'gz_0'=2,'gz_1'=2] {'gy_1'}, use_global_device_ids=true, to_apply=%region_15.16 | all-reduce | flops 2 | bytes 16 | tf_op jit(solution)/shard_map/psum | solution.py:34
  247.3 4.5 %all-reduce.13 = (f32[]{:T(128)}, f32[]{:T(128)}) all-reduce(f32[]{:T(128)} %get-tuple-element.32, f32[]{:T(128)} %get-tuple-element.33), channel_id=1, replica_groups=mesh['gx'=4,'gy_0'=4,'gy_1'=2,'gz_0'=2,'gz_1'=2] {'gz_0'}, use_global_device_ids=true, to_apply=%region_16.17 | all-reduce | flops 2 | bytes 16 | tf_op jit(solution)/shard_map/psum | solution.py:34
  251.7 13.7 %all-reduce.10 = (f32[]{:T(128)}, f32[]{:T(128)}) all-reduce(f32[]{:T(128)} %get-tuple-element.26, f32[]{:T(128)} %get-tuple-element.27), channel_id=1, replica_groups=mesh['gx'=4,'gy_0'=4,'gy_1'=2,'gz_0'=2,'gz_1'=2] {'gz_1'}, use_global_device_ids=true, to_apply=%region_17.18 | all-reduce | flops 2 | bytes 16 | tf_op jit(solution)/shard_map/psum | solution.py:34
  269.8 3.6 multiply_subtract_fusion.1
  273.4 3.3 convolution_select_fusion.7
  276.7 3.4 fusion.6
  280.2 3.4 fusion.5
  283.6 3.6 fusion.4
  287.2 3.4 fusion.3
  290.6 3.4 fusion.2
  294.1 3.4 fusion.1
  297.5 3.6 fusion.68
  303.8 3.3 collective-permute-start.8
  308.5 2.8 fusion.147
  317.6 5.5 %collective-permute-start.10 = (f32[64,66,1]{1,0,2:T(8,128)S(1)}, f32[64,66,1]{1,0,2:T(8,128)S(1)}, u32[]{:S(2)}, u32[]{:S(2)}) collective-permute-start(f32[64,66,1]{1,0,2:T(8,128)S(1)} %copy.157), channel_id=1, source_target_pairs={{0,4},{4,8},{8,12},{12,16},{16,20},{20,24},{24,28},{1,5},{5,9},{9,... | collective-permute-start | bytes 50696 | tf_op jit(solution)/shard_map/ppermute | solution.py:23
  327.6 6.4 %select_maximum_fusion = f32[66,66,130]{2,1,0:T(8,128)S(1)} fusion(f32[64,66,1]{2,1,0:T(8,128)} %copy.160, f32[64,66,1]{2,1,0:T(8,128)} %copy.159, f32[64,1,128]{2,1,0:T(1,128)S(1)} %bitcast.252, f32[64,64,128]{2,1,0:T(8,128)} %bitcast.238, f32[64,1,128]{2,1,0:T(1,128)S(1)} %bitcast.258), kind=kLoop, calls=%fused_computation.47 | loop fusion | flops 6795360 | bytes 4461600 | tf_op jit(solution)/shard_map/concatenate | solution.py:21
  334.1 6.0 %multiply_reduce_fusion = (f32[]{:T(128)}, f32[]{:T(128)}, f32[64,64,128]{2,1,0:T(8,128)}) fusion(f32[8,8,64,128]{3,2,1,0:T(8,128)S(1)} %copy-done.6, f32[64,64,128]{2,1,0:T(8,128)S(1)} %multiply_subtract_fusion.1, f32[64,1,128]{2,1,0:T(1,128)S(1)} %bitcast.253, f32[64,64,128]{2,1,0:T(8,128)S(1)} %bitcast.239, f32[64,1,128]{2,1,0:T(1,128)S(1)} %bitcast.259, ...), kind=kLoop, calls=%fused_computation.138 | loop fusion | flops 9961470 | bytes 14779400 | tf_op jit(solution)/shard_map/reduce_sum | solution.py:86
  340.1 6.6 %all-reduce.6 = (f32[]{:T(128)}, f32[]{:T(128)}) all-reduce(f32[]{:T(128)} %get-tuple-element.3, f32[]{:T(128)} %get-tuple-element.2), channel_id=1, replica_groups=mesh['gx'=4,'gy_0'=4,'gy_1'=2,'gz_0'=2,'gz_1'=2] {'gx'}, use_global_device_ids=true, to_apply=%region_25.26 | all-reduce | flops 2 | bytes 16 | tf_op jit(solution)/shard_map/psum | solution.py:34
  346.7 7.5 %all-reduce.3 = (f32[]{:T(128)}, f32[]{:T(128)}) all-reduce(f32[]{:T(128)} %get-tuple-element.12, f32[]{:T(128)} %get-tuple-element.13), channel_id=1, replica_groups=mesh['gx'=4,'gy_0'=4,'gy_1'=2,'gz_0'=2,'gz_1'=2] {'gy_0'}, use_global_device_ids=true, to_apply=%region_26.27 | all-reduce | flops 2 | bytes 16 | tf_op jit(solution)/shard_map/psum | solution.py:34
  354.2 5.9 %all-reduce.15 = (f32[]{:T(128)}, f32[]{:T(128)}) all-reduce(f32[]{:T(128)} %get-tuple-element.6, f32[]{:T(128)} %get-tuple-element.7), channel_id=1, replica_groups=mesh['gx'=4,'gy_0'=4,'gy_1'=2,'gz_0'=2,'gz_1'=2] {'gy_1'}, use_global_device_ids=true, to_apply=%region_27.28 | all-reduce | flops 2 | bytes 16 | tf_op jit(solution)/shard_map/psum | solution.py:34
  360.2 4.5 %all-reduce.12 = (f32[]{:T(128)}, f32[]{:T(128)}) all-reduce(f32[]{:T(128)} %get-tuple-element.30, f32[]{:T(128)} %get-tuple-element.31), channel_id=1, replica_groups=mesh['gx'=4,'gy_0'=4,'gy_1'=2,'gz_0'=2,'gz_1'=2] {'gz_0'}, use_global_device_ids=true, to_apply=%region_28.29 | all-reduce | flops 2 | bytes 16 | tf_op jit(solution)/shard_map/psum | solution.py:34
  364.6 13.5 %all-reduce.9 = (f32[]{:T(128)}, f32[]{:T(128)}) all-reduce(f32[]{:T(128)} %get-tuple-element.24, f32[]{:T(128)} %get-tuple-element.25), channel_id=1, replica_groups=mesh['gx'=4,'gy_0'=4,'gy_1'=2,'gz_0'=2,'gz_1'=2] {'gz_1'}, use_global_device_ids=true, to_apply=%region_29.30 | all-reduce | flops 2 | bytes 16 | tf_op jit(solution)/shard_map/psum | solution.py:34
  381.9 6.5 %multiply_subtract_fusion = (f32[64,64,128]{2,1,0:T(8,128)S(1)}, f32[64,64,128]{2,1,0:T(8,128)S(1)}) fusion(f32[64,64,128]{2,1,0:T(8,128)S(1)} %multiply_subtract_fusion.1, f32[64,64,128]{2,1,0:T(8,128)} %get-tuple-element.36, f32[]{:T(128)S(6)} %div.25, f32[]{:T(128)S(6)} %div.27, f32[64,64,128]{2,1,0:T(8,128)} %get-tuple-element.37, ...), kind=kLoop, calls=%fused_computation.136 | loop fusion | flops 7864320 | bytes 18874388 | tf_op jit(solution)/shard_map/sub | solution.py:105
  388.7 50.0 %all_to_all.45 = f32[64,64,256]{2,1,0:T(8,128)S(1)} all-to-all(f32[64,64,256]{2,1,0:T(8,128)S(1)} %pad_maximum_fusion), channel_id=1, replica_groups=mesh['gx'=4,'gy_0'=4,'gy_1'=2,'gz_0'=2,'gz_1'=2] {'gz_0','gz_1'}, dimensions={0} | all-to-all | bytes 8388608 | tf_op jit(solution)/shard_map/all_to_all | solution.py:46
  (85 shorter events, 52.7 us)
Async XLA Ops:
  4.8 29.7 %all-to-all-start = ((f32[16,256,128]{2,0,1:T(8,128)}), f32[16,256,128]{2,0,1:T(8,128)S(1)}, u32[]{:S(2)}, u32[]{:S(2)}) async-start(f32[16,256,128]{2,0,1:T(8,128)} %copy.125), calls=%async_computation | async-start | bytes 4194304 | tf_op jit(solution)/shard_map/all_to_all | solution.py:92
  34.4 5.9 %copy-start.16 = (f32[16,256,128]{2,0,1:T(8,128)}, f32[16,256,128]{2,0,1:T(8,128)S(1)}, u32[]{:S(2)}) copy-start(f32[16,256,128]{2,0,1:T(8,128)S(1)} %all-to-all-done) | copy-start | bytes 6291460
  34.4 38.7 %all-to-all-start.1 = ((f32[16,256,128]{2,0,1:T(8,128)}), f32[16,256,128]{2,0,1:T(8,128)}, u32[]{:S(2)}, u32[]{:S(2)}) async-start(f32[16,256,128]{2,0,1:T(8,128)} %copy.127), calls=%async_computation.1 | async-start | bytes 4194304 | tf_op jit(solution)/shard_map/all_to_all | solution.py:93
  40.3 1.0 copy-start.18
  41.0 22.7 %copy-start.1 = (f32[16,4,64,128]{3,2,0,1:T(8,128)}, f32[16,4,64,128]{3,2,0,1:T(8,128)S(1)}, u32[]{:S(2)}) copy-start(f32[16,4,64,128]{3,2,0,1:T(8,128)S(1)} %copy.126) | copy-start | bytes 6291460
  67.5 37.9 %copy-start.2 = (f32[8,8,64,128]{3,2,1,0:T(8,128)}, f32[8,8,64,128]{3,2,1,0:T(8,128)S(1)}, u32[]{:S(2)}) copy-start(f32[8,8,64,128]{3,2,1,0:T(8,128)S(1)} %copy.167) | copy-start | bytes 6291460
  67.6 8.6 %collective-permute-start.1 = (f32[64,1,128]{2,0,1:T(8,128)S(1)}, f32[64,1,128]{2,0,1:T(8,128)S(1)}, u32[]{:S(2)}, u32[]{:S(2)}) collective-permute-start(f32[64,1,128]{2,0,1:T(8,128)S(1)} %bitcast.264), channel_id=1, source_target_pairs={{1,0},{2,1},{3,2},{32,3},{33,32},{34,33},{35,34},{64,35},{65,64},{... | collective-permute-start | bytes 98312 | tf_op jit(solution)/shard_map/ppermute | solution.py:25
  69.6 6.7 %collective-permute-start = (f32[64,1,128]{2,0,1:T(8,128)S(1)}, f32[64,1,128]{2,0,1:T(8,128)S(1)}, u32[]{:S(2)}, u32[]{:S(2)}) collective-permute-start(f32[64,1,128]{2,0,1:T(8,128)S(1)} %bitcast.263), channel_id=1, source_target_pairs={{0,1},{1,2},{2,3},{3,32},{32,33},{33,34},{34,35},{35,64},{64,65},{... | collective-permute-start | bytes 98312 | tf_op jit(solution)/shard_map/ppermute | solution.py:23
  84.3 13.4 %collective-permute-start.2 = (f32[64,66,1]{1,0,2:T(8,128)S(1)}, f32[64,66,1]{1,0,2:T(8,128)S(1)}, u32[]{:S(2)}, u32[]{:S(2)}) collective-permute-start(f32[64,66,1]{1,0,2:T(8,128)S(1)} %copy.133), channel_id=1, source_target_pairs={{0,4},{4,8},{8,12},{12,16},{16,20},{20,24},{24,28},{1,5},{5,9},{9,... | collective-permute-start | bytes 50696 | tf_op jit(solution)/shard_map/ppermute | solution.py:23
  89.1 6.4 %collective-permute-start.3 = (f32[64,66,1]{1,0,2:T(8,128)S(1)}, f32[64,66,1]{1,0,2:T(8,128)S(1)}, u32[]{:S(2)}, u32[]{:S(2)}) collective-permute-start(f32[64,66,1]{1,0,2:T(8,128)S(1)} %copy.134), channel_id=1, source_target_pairs={{4,0},{8,4},{12,8},{16,12},{20,16},{24,20},{28,24},{5,1},{9,5},{13... | collective-permute-start | bytes 50696 | tf_op jit(solution)/shard_map/ppermute | solution.py:25
  90.4 3.1 copy-start.17
  100.0 5.5 %copy-start.7 = (f32[16,4,64,128]{3,2,0,1:T(8,128)S(1)}, f32[16,4,64,128]{3,2,0,1:T(8,128)}, u32[]{:S(2)}) copy-start(f32[16,4,64,128]{3,2,0,1:T(8,128)} %copy.128) | copy-start | bytes 6291460
  100.0 5.5 %copy-start.12 = (f32[64,66,1]{2,1,0:T(8,128)S(1)}, f32[64,66,1]{2,1,0:T(8,128)}, u32[]{:S(2)}) copy-start(f32[64,66,1]{2,1,0:T(8,128)} %copy.136) | copy-start | bytes 50692
  100.0 5.5 %copy-start.15 = (f32[64,66,1]{2,1,0:T(8,128)S(1)}, f32[64,66,1]{2,1,0:T(8,128)}, u32[]{:S(2)}) copy-start(f32[64,66,1]{2,1,0:T(8,128)} %copy.135) | copy-start | bytes 50692
  158.5 60.4 %copy-start = (f32[64,64,128]{2,1,0:T(8,128)}, f32[64,64,128]{2,1,0:T(8,128)S(1)}, u32[]{:S(2)}) copy-start(f32[64,64,128]{2,1,0:T(8,128)S(1)} %bitcast_subtract_fusion) | copy-start | bytes 6291460
  186.5 6.6 %copy-start.3 = (f32[8,8,64,128]{3,2,1,0:T(8,128)}, f32[8,8,64,128]{3,2,1,0:T(8,128)S(1)}, u32[]{:S(2)}) copy-start(f32[8,8,64,128]{3,2,1,0:T(8,128)S(1)} %copy.170) | copy-start | bytes 6291460
  186.6 5.6 %collective-permute-start.5 = (f32[64,1,128]{2,0,1:T(8,128)S(1)}, f32[64,1,128]{2,0,1:T(8,128)S(1)}, u32[]{:S(2)}, u32[]{:S(2)}) collective-permute-start(f32[64,1,128]{2,0,1:T(8,128)S(1)} %bitcast.267), channel_id=1, source_target_pairs={{1,0},{2,1},{3,2},{32,3},{33,32},{34,33},{35,34},{64,35},{65,64},{... | collective-permute-start | bytes 98312 | tf_op jit(solution)/shard_map/ppermute | solution.py:25
  188.9 4.3 collective-permute-start.4
  198.9 9.3 %collective-permute-start.7 = (f32[64,66,1]{1,0,2:T(8,128)S(1)}, f32[64,66,1]{1,0,2:T(8,128)S(1)}, u32[]{:S(2)}, u32[]{:S(2)}) collective-permute-start(f32[64,66,1]{1,0,2:T(8,128)S(1)} %copy.146), channel_id=1, source_target_pairs={{4,0},{8,4},{12,8},{16,12},{20,16},{24,20},{28,24},{5,1},{9,5},{13... | collective-permute-start | bytes 50696 | tf_op jit(solution)/shard_map/ppermute | solution.py:25
  202.6 7.8 %collective-permute-start.6 = (f32[64,66,1]{1,0,2:T(8,128)S(1)}, f32[64,66,1]{1,0,2:T(8,128)S(1)}, u32[]{:S(2)}, u32[]{:S(2)}) collective-permute-start(f32[64,66,1]{1,0,2:T(8,128)S(1)} %copy.145), channel_id=1, source_target_pairs={{0,4},{4,8},{8,12},{12,16},{16,20},{20,24},{24,28},{1,5},{5,9},{9,... | collective-permute-start | bytes 50696 | tf_op jit(solution)/shard_map/ppermute | solution.py:23
  212.6 6.2 %copy-start.4 = (f32[8,8,64,128]{3,2,1,0:T(8,128)S(1)}, f32[8,8,64,128]{3,2,1,0:T(8,128)}, u32[]{:S(2)}) copy-start(f32[8,8,64,128]{3,2,1,0:T(8,128)} %copy-done.3) | copy-start | bytes 6291460
  212.6 6.2 %copy-start.8 = (f32[16,4,64,128]{3,2,0,1:T(8,128)S(1)}, f32[16,4,64,128]{3,2,0,1:T(8,128)}, u32[]{:S(2)}) copy-start(f32[16,4,64,128]{3,2,0,1:T(8,128)} %copy.128) | copy-start | bytes 6291460
  212.6 6.2 %copy-start.11 = (f32[64,66,1]{2,1,0:T(8,128)S(1)}, f32[64,66,1]{2,1,0:T(8,128)}, u32[]{:S(2)}) copy-start(f32[64,66,1]{2,1,0:T(8,128)} %copy.148) | copy-start | bytes 50692
  212.7 6.2 %copy-start.14 = (f32[64,66,1]{2,1,0:T(8,128)S(1)}, f32[64,66,1]{2,1,0:T(8,128)}, u32[]{:S(2)}) copy-start(f32[64,66,1]{2,1,0:T(8,128)} %copy.147) | copy-start | bytes 50692
  301.5 6.7 %copy-start.5 = (f32[8,8,64,128]{3,2,1,0:T(8,128)}, f32[8,8,64,128]{3,2,1,0:T(8,128)S(1)}, u32[]{:S(2)}) copy-start(f32[8,8,64,128]{3,2,1,0:T(8,128)S(1)} %copy.172) | copy-start | bytes 6291460
  301.6 5.6 %collective-permute-start.9 = (f32[64,1,128]{2,0,1:T(8,128)S(1)}, f32[64,1,128]{2,0,1:T(8,128)S(1)}, u32[]{:S(2)}, u32[]{:S(2)}) collective-permute-start(f32[64,1,128]{2,0,1:T(8,128)S(1)} %bitcast.268), channel_id=1, source_target_pairs={{1,0},{2,1},{3,2},{32,3},{33,32},{34,33},{35,34},{64,35},{65,64},{... | collective-permute-start | bytes 98312 | tf_op jit(solution)/shard_map/ppermute | solution.py:25
  303.8 4.3 collective-permute-start.8
  313.8 9.3 %collective-permute-start.11 = (f32[64,66,1]{1,0,2:T(8,128)S(1)}, f32[64,66,1]{1,0,2:T(8,128)S(1)}, u32[]{:S(2)}, u32[]{:S(2)}) collective-permute-start(f32[64,66,1]{1,0,2:T(8,128)S(1)} %copy.158), channel_id=1, source_target_pairs={{4,0},{8,4},{12,8},{16,12},{20,16},{24,20},{28,24},{5,1},{9,5},{13... | collective-permute-start | bytes 50696 | tf_op jit(solution)/shard_map/ppermute | solution.py:25
  317.6 7.8 %collective-permute-start.10 = (f32[64,66,1]{1,0,2:T(8,128)S(1)}, f32[64,66,1]{1,0,2:T(8,128)S(1)}, u32[]{:S(2)}, u32[]{:S(2)}) collective-permute-start(f32[64,66,1]{1,0,2:T(8,128)S(1)} %copy.157), channel_id=1, source_target_pairs={{0,4},{4,8},{8,12},{12,16},{16,20},{20,24},{24,28},{1,5},{5,9},{9,... | collective-permute-start | bytes 50696 | tf_op jit(solution)/shard_map/ppermute | solution.py:23
  327.6 6.4 %copy-start.6 = (f32[8,8,64,128]{3,2,1,0:T(8,128)S(1)}, f32[8,8,64,128]{3,2,1,0:T(8,128)}, u32[]{:S(2)}) copy-start(f32[8,8,64,128]{3,2,1,0:T(8,128)} %copy-done.5) | copy-start | bytes 6291460
  327.6 6.4 %copy-start.9 = (f32[16,4,64,128]{3,2,0,1:T(8,128)S(1)}, f32[16,4,64,128]{3,2,0,1:T(8,128)}, u32[]{:S(2)}) copy-start(f32[16,4,64,128]{3,2,0,1:T(8,128)} %copy.128) | copy-start | bytes 6291460
  327.6 6.4 %copy-start.10 = (f32[64,66,1]{2,1,0:T(8,128)S(1)}, f32[64,66,1]{2,1,0:T(8,128)}, u32[]{:S(2)}) copy-start(f32[64,66,1]{2,1,0:T(8,128)} %copy.160) | copy-start | bytes 50692
  327.6 6.4 %copy-start.13 = (f32[64,66,1]{2,1,0:T(8,128)S(1)}, f32[64,66,1]{2,1,0:T(8,128)}, u32[]{:S(2)}) copy-start(f32[64,66,1]{2,1,0:T(8,128)} %copy.159) | copy-start | bytes 50692
where the time goes:
time: 446 us; the launch traced here: 442 us
  blocking collectives  172 us (39%)
  matrix products  81.1 us (18%)
  other arithmetic  56.9 us (13%)
  local copies, waits for them, and re-layouts  52.2 us (12%)
  starting transfers between devices  47.2 us (11%)
  waiting for transfers between devices  21.8 us (5%)
  between operations  10.9 us (2%)
    psum x15, blocking collectives, over_axes(): x = lax.psum(x, axis)  122 us
    dot_general x24, matrix products, apply_blocks(): jnp.dot(matrices[member], flattened, precision=lax.Precision.HIGHEST)  81.1 us
    all_to_all x1, blocking collectives, sent_together(): lax.all_to_all(both, axis, split_axis=split_dim, concat_axis=concat_dim,...  50 us
    ppermute x6, starting transfers between devices, extended(): lax.ppermute(tail, axis, [(i, (i + 1) % count) for i in range(ends)])  26 us
    all_to_all x1, waiting for transfers between devices, per_device(): lax.all_to_all(right_side, GZ, split_axis=1, concat_axis=0, tiled=True)  19.8 us
    concatenate x6, other arithmetic, extended(): jnp.concatenate([lax.ppermute(tail, axis, [(i, (i + 1) % count) for i in...  19.1 us
    reduce_sum x3, other arithmetic, paired(): jnp.sum(image * precond)  17.7 us
    slice x6, local copies, waits for them, and re-layouts, extended(): head = lax.slice_in_dim(cells, 0, width, axis=dim)  15.9 us
  transfers between devices with their start and end apart: 14, of which 3 were waited for; matrix products, arithmetic and copies ran while one was open for 12% of the time, Pallas kernels for 0%

commit v1 on v0

--- a/solution.py
+++ b/solution.py
@@ -31,7 +31,7 @@
 
 def over_axes(x, axes):
     for axis in axes:
-        x = lax.psum(x, axis)
+        x = jnp.sum(lax.all_gather(x, axis), axis=0)
     return x
 
 

time: 446 us -> 496 us (1.11)
  local copies, waits for them, and re-layouts: 52.2 us -> 96.6 us
  blocking collectives: 172 us -> 152 us
  other arithmetic: 56.9 us -> 76.2 us
  waiting for transfers between devices: 21.8 us -> 30.7 us
    psum x15 -> x0, blocking collectives: 122 us -> none  [over_axes(): x = lax.psum(x, axis)]
    unnamed x0 -> x15, blocking collectives: none -> 102 us
    unnamed x43 -> x118, local copies, waits for them, and re-layouts: 9.73 us -> 54.1 us
    reduce_sum x0 -> x30, other arithmetic: none -> 19.5 us  [over_axes(): x = jnp.sum(lax.all_gather(x, axis), axis=0)]
    ppermute x6, waiting for transfers between devices: 0.02 us -> 11.5 us  [extended(): lax.ppermute(head, axis, [((i + 1) % count, i) for i in range(ends)])]
  transfers between devices with their start and end apart: 14 -> 14, of which waited for: 3 -> 6; matrix products, arithmetic and copies ran while one was open for 12% -> 11% of each run, Pallas kernels for 0% -> 0%
where the time goes in v1:
time: 496 us; the launch traced here: 491 us
  blocking collectives  152 us (31%)
  local copies, waits for them, and re-layouts  96.6 us (19%)
  matrix products  81.5 us (16%)
  other arithmetic  76.2 us (15%)
  starting transfers between devices  42.9 us (9%)
  waiting for transfers between devices  30.7 us (6%)
  between operations  11.4 us (2%)
    unnamed x15, blocking collectives  102 us
    dot_general x24, matrix products, apply_blocks(): jnp.dot(matrices[member], flattened, precision=lax.Precision.HIGHEST)  81.5 us
    unnamed x118, local copies, waits for them, and re-layouts  54.1 us
    all_to_all x1, blocking collectives, sent_together(): lax.all_to_all(both, axis, split_axis=split_dim, concat_axis=concat_dim,...  50 us
    ppermute x6, starting transfers between devices, extended(): lax.ppermute(tail, axis, [(i, (i + 1) % count) for i in range(ends)])  22.3 us
    reduce_sum x30, other arithmetic, over_axes(): x = jnp.sum(lax.all_gather(x, axis), axis=0)  19.5 us
    all_to_all x1, waiting for transfers between devices, per_device(): lax.all_to_all(right_side, GZ, split_axis=1, concat_axis=0, tiled=True)  19.1 us
    concatenate x6, other arithmetic, extended(): jnp.concatenate([lax.ppermute(tail, axis, [(i, (i + 1) % count) for i in...  19 us
  transfers between devices with their start and end apart: 14, of which 6 were waited for; matrix products, arithmetic and copies ran while one was open for 11% of the time, Pallas kernels for 0%

profile of v1, /device:TPU:1, one launch (start us, length us, event | category | flops | bytes accessed | tf_op | source)
XLA Modules:
  0.0 491.0 jit_solution(13610078496204365989)
XLA Ops:
  0.6 4.1 copy.125
  4.8 5.0 %all-to-all-start = ((f32[16,256,128]{2,0,1:T(8,128)}), f32[16,256,128]{2,0,1:T(8,128)S(1)}, u32[]{:S(2)}, u32[]{:S(2)}) async-start(f32[16,256,128]{2,0,1:T(8,128)} %copy.125), calls=%async_computation | async-start | bytes 4194304 | tf_op jit(solution)/shard_map/all_to_all | solution.py:92
  9.7 4.1 copy.127
  15.3 19.1 %all-to-all-done = f32[16,256,128]{2,0,1:T(8,128)S(1)} async-done(((f32[16,256,128]{2,0,1:T(8,128)}), f32[16,256,128]{2,0,1:T(8,128)S(1)}, u32[]{:S(2)}, u32[]{:S(2)}) %all-to-all-start) | async-done | bytes 2097184 | tf_op jit(solution)/shard_map/all_to_all | solution.py:92
  34.4 5.5 %all-to-all-start.1 = ((f32[16,256,128]{2,0,1:T(8,128)}), f32[16,256,128]{2,0,1:T(8,128)}, u32[]{:S(2)}, u32[]{:S(2)}) async-start(f32[16,256,128]{2,0,1:T(8,128)} %copy.127), calls=%async_computation.1 | async-start | bytes 4194304 | tf_op jit(solution)/shard_map/all_to_all | solution.py:93
  40.9 3.1 convolution_select_fusion.23
  44.0 3.2 fusion.20
  47.2 3.2 fusion.19
  50.4 3.4 fusion.18
  53.8 3.2 fusion.17
  57.0 3.2 fusion.16
  60.2 3.2 fusion.15
  63.4 3.6 fusion.62
  67.4 3.5 collective-permute-start
  72.9 3.0 broadcast_add_fusion
  76.6 2.8 fusion.149
  81.9 4.8 collective-permute-start.2
  90.4 3.1 fusion.38
  101.4 5.4 %select_maximum_fusion.8 = f32[66,66,130]{2,1,0:T(8,128)S(1)} fusion(f32[64,66,1]{2,1,0:T(8,128)} %copy.136, f32[64,66,1]{2,1,0:T(8,128)} %copy.135, f32[64,1,128]{2,1,0:T(1,128)S(1)} %bitcast.284, f32[64,64,128]{2,1,0:T(8,128)S(1)} %bitcast.265, f32[64,1,128]{2,1,0:T(1,128)S(1)} %bitcast.281), kind=kLoop, calls=%fused_computation.55 | loop fusion | flops 6795360 | bytes 4461600 | tf_op jit(solution)/shard_map/concatenate | solution.py:21
  106.9 5.7 %multiply_reduce_fusion.4 = (f32[]{:T(128)}, f32[64,64,128]{2,1,0:T(8,128)}) fusion(f32[8,8,64,128]{3,2,1,0:T(8,128)S(1)} %copy.167, f32[64,1,128]{2,1,0:T(1,128)S(1)} %bitcast.285, f32[64,64,128]{2,1,0:T(8,128)S(1)} %bitcast.266, f32[64,1,128]{2,1,0:T(1,128)S(1)} %bitcast.282, f32[64,66,1]{2,1,0:T(8,128)S(1)} %copy-done.12, ...), kind=kLoop, calls=%fused_computation.144 | loop fusion | flops 8912895 | bytes 12682244 | tf_op jit(solution)/shard_map/reduce_sum | solution.py:86
  114.5 8.7 %all-reduce.38 = (f32[4]{0:T(128)S(1)}, f32[4]{0:T(128)S(1)}) all-reduce(f32[4]{0:T(128)S(1)} %dynamic-update-slice, f32[4]{0:T(128)S(1)} %dynamic-update-slice.5), channel_id=1, replica_groups=mesh['gx'=4,'gy_0'=4,'gy_1'=2,'gz_0'=2,'gz_1'=2] {'gx'}, use_global_device_ids=true, to_apply=%add.3 | all-reduce | flops 8 | bytes 64
  127.7 11.5 %all-reduce.35 = (f32[4]{0:T(128)S(1)}, f32[4]{0:T(128)S(1)}) all-reduce(f32[4]{0:T(128)S(1)} %dynamic-update-slice.1, f32[4]{0:T(128)S(1)} %dynamic-update-slice.6), channel_id=1, replica_groups=mesh['gx'=4,'gy_0'=4,'gy_1'=2,'gz_0'=2,'gz_1'=2] {'gy_0'}, use_global_device_ids=true, to_apply=%add.4 | all-reduce | flops 8 | bytes 64
  143.8 5.3 %all-reduce.47 = (f32[2]{0:T(128)S(1)}, f32[2]{0:T(128)S(1)}) all-reduce(f32[2]{0:T(128)S(1)} %dynamic-update-slice.2, f32[2]{0:T(128)S(1)} %dynamic-update-slice.7), channel_id=1, replica_groups=mesh['gx'=4,'gy_0'=4,'gy_1'=2,'gz_0'=2,'gz_1'=2] {'gy_1'}, use_global_device_ids=true, to_apply=%add.5 | all-reduce | flops 4 | bytes 32
  153.7 3.8 all-reduce.44
  161.6 10.0 %all-reduce.41 = (f32[2]{0:T(128)S(1)}, f32[2]{0:T(128)S(1)}) all-reduce(f32[2]{0:T(128)S(1)} %dynamic-update-slice.4, f32[2]{0:T(128)S(1)} %dynamic-update-slice.9), channel_id=1, replica_groups=mesh['gx'=4,'gy_0'=4,'gy_1'=2,'gz_0'=2,'gz_1'=2] {'gz_1'}, use_global_device_ids=true, to_apply=%add.7 | all-reduce | flops 4 | bytes 32
  177.0 3.3 convolution_select_fusion.15
  180.3 3.4 fusion.13
  183.7 3.4 fusion.12
  187.2 3.8 fusion.11
  191.0 3.4 fusion.10
  194.4 3.4 fusion.9
  197.8 3.4 fusion.8
  201.3 3.6 fusion.65
  205.3 2.9 collective-permute-start.4
  210.2 3.3 collective-permute-done.5
  213.9 2.8 fusion.148
  219.2 3.8 collective-permute-start.6
  233.8 6.2 %select_maximum_fusion.4 = f32[66,66,130]{2,1,0:T(8,128)S(1)} fusion(f32[64,66,1]{2,1,0:T(8,128)} %copy.148, f32[64,66,1]{2,1,0:T(8,128)} %copy.147, f32[64,1,128]{2,1,0:T(1,128)S(1)} %bitcast.296, f32[64,64,128]{2,1,0:T(8,128)} %bitcast.269, f32[64,1,128]{2,1,0:T(1,128)S(1)} %bitcast.290), kind=kLoop, calls=%fused_computation.51 | loop fusion | flops 6795360 | bytes 4461600 | tf_op jit(solution)/shard_map/concatenate | solution.py:21
  240.1 6.0 %multiply_reduce_fusion.2 = (f32[]{:T(128)}, f32[]{:T(128)}, f32[64,64,128]{2,1,0:T(8,128)}) fusion(f32[8,8,64,128]{3,2,1,0:T(8,128)S(1)} %copy-done.4, f32[64,64,128]{2,1,0:T(8,128)S(1)} %bitcast_subtract_fusion, f32[64,1,128]{2,1,0:T(1,128)S(1)} %bitcast.297, f32[64,64,128]{2,1,0:T(8,128)S(1)} %bitcast.270, f32[64,1,128]{2,1,0:T(1,128)S(1)} %bitcast.291, ...), kind=kLoop, calls=%fused_computation.142 | loop fusion | flops 9961470 | bytes 14779400 | tf_op jit(solution)/shard_map/reduce_sum | solution.py:86
  248.9 6.0 %all-reduce.37 = (f32[4]{0:T(128)S(1)}, f32[4]{0:T(128)S(1)}) all-reduce(f32[4]{0:T(128)S(1)} %dynamic-update-slice.10, f32[4]{0:T(128)S(1)} %dynamic-update-slice.15), channel_id=1, replica_groups=mesh['gx'=4,'gy_0'=4,'gy_1'=2,'gz_0'=2,'gz_1'=2] {'gx'}, use_global_device_ids=true, to_apply=%add.13 | all-reduce | flops 8 | bytes 64
  258.8 6.0 %all-reduce.34 = (f32[4]{0:T(128)S(1)}, f32[4]{0:T(128)S(1)}) all-reduce(f32[4]{0:T(128)S(1)} %dynamic-update-slice.11, f32[4]{0:T(128)S(1)} %dynamic-update-slice.16), channel_id=1, replica_groups=mesh['gx'=4,'gy_0'=4,'gy_1'=2,'gz_0'=2,'gz_1'=2] {'gy_0'}, use_global_device_ids=true, to_apply=%add.14 | all-reduce | flops 8 | bytes 64
  268.8 5.3 %all-reduce.46 = (f32[2]{0:T(128)S(1)}, f32[2]{0:T(128)S(1)}) all-reduce(f32[2]{0:T(128)S(1)} %dynamic-update-slice.12, f32[2]{0:T(128)S(1)} %dynamic-update-slice.17), channel_id=1, replica_groups=mesh['gx'=4,'gy_0'=4,'gy_1'=2,'gz_0'=2,'gz_1'=2] {'gy_1'}, use_global_device_ids=true, to_apply=%add.15 | all-reduce | flops 4 | bytes 32
  278.0 3.8 all-reduce.43
  286.3 9.3 %all-reduce.40 = (f32[2]{0:T(128)S(1)}, f32[2]{0:T(128)S(1)}) all-reduce(f32[2]{0:T(128)S(1)} %dynamic-update-slice.14, f32[2]{0:T(128)S(1)} %dynamic-update-slice.19), channel_id=1, replica_groups=mesh['gx'=4,'gy_0'=4,'gy_1'=2,'gz_0'=2,'gz_1'=2] {'gz_1'}, use_global_device_ids=true, to_apply=%add.17 | all-reduce | flops 4 | bytes 32
  301.5 3.6 multiply_subtract_fusion.1
  305.1 3.3 convolution_select_fusion.7
  308.4 3.4 fusion.6
  311.8 3.4 fusion.5
  315.3 3.6 fusion.4
  318.9 3.4 fusion.3
  322.3 3.4 fusion.2
  325.7 3.4 fusion.1
  329.2 3.6 fusion.68
  340.8 2.8 fusion.147
  346.1 5.4 %collective-permute-start.10 = (f32[64,66,1]{1,0,2:T(8,128)S(1)}, f32[64,66,1]{1,0,2:T(8,128)S(1)}, u32[]{:S(2)}, u32[]{:S(2)}) collective-permute-start(f32[64,66,1]{1,0,2:T(8,128)S(1)} %copy.157), channel_id=1, source_target_pairs={{0,4},{4,8},{8,12},{12,16},{16,20},{20,24},{24,28},{1,5},{5,9},{9,... | collective-permute-start | bytes 50696 | tf_op jit(solution)/shard_map/ppermute | solution.py:23
  362.3 6.2 %select_maximum_fusion = f32[66,66,130]{2,1,0:T(8,128)S(1)} fusion(f32[64,66,1]{2,1,0:T(8,128)} %copy.160, f32[64,66,1]{2,1,0:T(8,128)} %copy.159, f32[64,1,128]{2,1,0:T(1,128)S(1)} %bitcast.293, f32[64,64,128]{2,1,0:T(8,128)} %bitcast.273, f32[64,1,128]{2,1,0:T(1,128)S(1)} %bitcast.287), kind=kLoop, calls=%fused_computation.47 | loop fusion | flops 6795360 | bytes 4461600 | tf_op jit(solution)/shard_map/concatenate | solution.py:21
  368.6 6.0 %multiply_reduce_fusion = (f32[]{:T(128)}, f32[]{:T(128)}, f32[64,64,128]{2,1,0:T(8,128)}) fusion(f32[8,8,64,128]{3,2,1,0:T(8,128)S(1)} %copy-done.6, f32[64,64,128]{2,1,0:T(8,128)S(1)} %multiply_subtract_fusion.1, f32[64,1,128]{2,1,0:T(1,128)S(1)} %bitcast.294, f32[64,64,128]{2,1,0:T(8,128)S(1)} %bitcast.274, f32[64,1,128]{2,1,0:T(1,128)S(1)} %bitcast.288, ...), kind=kLoop, calls=%fused_computation.138 | loop fusion | flops 9961470 | bytes 14779400 | tf_op jit(solution)/shard_map/reduce_sum | solution.py:86
  377.3 8.3 %all-reduce.36 = (f32[4]{0:T(128)S(1)}, f32[4]{0:T(128)S(1)}) all-reduce(f32[4]{0:T(128)S(1)} %dynamic-update-slice.20, f32[4]{0:T(128)S(1)} %dynamic-update-slice.25), channel_id=1, replica_groups=mesh['gx'=4,'gy_0'=4,'gy_1'=2,'gz_0'=2,'gz_1'=2] {'gx'}, use_global_device_ids=true, to_apply=%add.23 | all-reduce | flops 8 | bytes 64
  389.5 6.1 %all-reduce.33 = (f32[4]{0:T(128)S(1)}, f32[4]{0:T(128)S(1)}) all-reduce(f32[4]{0:T(128)S(1)} %dynamic-update-slice.21, f32[4]{0:T(128)S(1)} %dynamic-update-slice.26), channel_id=1, replica_groups=mesh['gx'=4,'gy_0'=4,'gy_1'=2,'gz_0'=2,'gz_1'=2] {'gy_0'}, use_global_device_ids=true, to_apply=%add.24 | all-reduce | flops 8 | bytes 64
  399.5 5.3 %all-reduce.45 = (f32[2]{0:T(128)S(1)}, f32[2]{0:T(128)S(1)}) all-reduce(f32[2]{0:T(128)S(1)} %dynamic-update-slice.22, f32[2]{0:T(128)S(1)} %dynamic-update-slice.27), channel_id=1, replica_groups=mesh['gx'=4,'gy_0'=4,'gy_1'=2,'gz_0'=2,'gz_1'=2] {'gy_1'}, use_global_device_ids=true, to_apply=%add.25 | all-reduce | flops 4 | bytes 32
  408.9 3.8 all-reduce.42
  416.8 8.8 %all-reduce.39 = (f32[2]{0:T(128)S(1)}, f32[2]{0:T(128)S(1)}) all-reduce(f32[2]{0:T(128)S(1)} %dynamic-update-slice.24, f32[2]{0:T(128)S(1)} %dynamic-update-slice.29), channel_id=1, replica_groups=mesh['gx'=4,'gy_0'=4,'gy_1'=2,'gz_0'=2,'gz_1'=2] {'gz_1'}, use_global_device_ids=true, to_apply=%add.27 | all-reduce | flops 4 | bytes 32
  430.8 6.5 %multiply_subtract_fusion = (f32[64,64,128]{2,1,0:T(8,128)S(1)}, f32[64,64,128]{2,1,0:T(8,128)S(1)}) fusion(f32[64,64,128]{2,1,0:T(8,128)S(1)} %multiply_subtract_fusion.1, f32[64,64,128]{2,1,0:T(8,128)} %get-tuple-element.36, f32[]{:T(128)S(6)} %div.25, f32[]{:T(128)S(6)} %div.27, f32[64,64,128]{2,1,0:T(8,128)} %get-tuple-element.37, ...), kind=kLoop, calls=%fused_computation.136 | loop fusion | flops 7864320 | bytes 18874388 | tf_op jit(solution)/shard_map/sub | solution.py:105
  437.7 50.0 %all_to_all.45 = f32[64,64,256]{2,1,0:T(8,128)S(1)} all-to-all(f32[64,64,256]{2,1,0:T(8,128)S(1)} %pad_maximum_fusion), channel_id=1, replica_groups=mesh['gx'=4,'gy_0'=4,'gy_1'=2,'gz_0'=2,'gz_1'=2] {'gz_0','gz_1'}, dimensions={0} | all-to-all | bytes 8388608 | tf_op jit(solution)/shard_map/all_to_all | solution.py:46
  (190 shorter events, 124.5 us)
Async XLA Ops:
  4.8 29.7 %all-to-all-start = ((f32[16,256,128]{2,0,1:T(8,128)}), f32[16,256,128]{2,0,1:T(8,128)S(1)}, u32[]{:S(2)}, u32[]{:S(2)}) async-start(f32[16,256,128]{2,0,1:T(8,128)} %copy.125), calls=%async_computation | async-start | bytes 4194304 | tf_op jit(solution)/shard_map/all_to_all | solution.py:92
  9.7 4.1 copy-start.23
  34.4 5.5 %copy-start.16 = (f32[16,256,128]{2,0,1:T(8,128)}, f32[16,256,128]{2,0,1:T(8,128)S(1)}, u32[]{:S(2)}) copy-start(f32[16,256,128]{2,0,1:T(8,128)S(1)} %all-to-all-done) | copy-start | bytes 6291460
  34.4 38.5 %all-to-all-start.1 = ((f32[16,256,128]{2,0,1:T(8,128)}), f32[16,256,128]{2,0,1:T(8,128)}, u32[]{:S(2)}, u32[]{:S(2)}) async-start(f32[16,256,128]{2,0,1:T(8,128)} %copy.127), calls=%async_computation.1 | async-start | bytes 4194304 | tf_op jit(solution)/shard_map/all_to_all | solution.py:93
  40.0 1.0 copy-start.18
  40.6 22.8 %copy-start.1 = (f32[16,4,64,128]{3,2,0,1:T(8,128)}, f32[16,4,64,128]{3,2,0,1:T(8,128)S(1)}, u32[]{:S(2)}) copy-start(f32[16,4,64,128]{3,2,0,1:T(8,128)S(1)} %copy.126) | copy-start | bytes 6291460
  67.4 39.4 %copy-start.2 = (f32[8,8,64,128]{3,2,1,0:T(8,128)}, f32[8,8,64,128]{3,2,1,0:T(8,128)S(1)}, u32[]{:S(2)}) copy-start(f32[8,8,64,128]{3,2,1,0:T(8,128)S(1)} %copy.167) | copy-start | bytes 6291460
  67.4 8.5 %collective-permute-start = (f32[64,1,128]{2,0,1:T(8,128)S(1)}, f32[64,1,128]{2,0,1:T(8,128)S(1)}, u32[]{:S(2)}, u32[]{:S(2)}) collective-permute-start(f32[64,1,128]{2,0,1:T(8,128)S(1)} %bitcast.299), channel_id=1, source_target_pairs={{0,1},{1,2},{2,3},{3,32},{32,33},{33,34},{34,35},{35,64},{64,65},{... | collective-permute-start | bytes 98312 | tf_op jit(solution)/shard_map/ppermute | solution.py:23
  71.0 5.2 %collective-permute-start.1 = (f32[64,1,128]{2,0,1:T(8,128)S(1)}, f32[64,1,128]{2,0,1:T(8,128)S(1)}, u32[]{:S(2)}, u32[]{:S(2)}) collective-permute-start(f32[64,1,128]{2,0,1:T(8,128)S(1)} %bitcast.298), channel_id=1, source_target_pairs={{1,0},{2,1},{3,2},{32,3},{33,32},{34,33},{35,34},{64,35},{65,64},{... | collective-permute-start | bytes 98312 | tf_op jit(solution)/shard_map/ppermute | solution.py:25
  81.9 15.0 %collective-permute-start.2 = (f32[64,66,1]{1,0,2:T(8,128)S(1)}, f32[64,66,1]{1,0,2:T(8,128)S(1)}, u32[]{:S(2)}, u32[]{:S(2)}) collective-permute-start(f32[64,66,1]{1,0,2:T(8,128)S(1)} %copy.133), channel_id=1, source_target_pairs={{0,4},{4,8},{8,12},{12,16},{16,20},{20,24},{24,28},{1,5},{5,9},{9,... | collective-permute-start | bytes 50696 | tf_op jit(solution)/shard_map/ppermute | solution.py:23
  89.1 10.0 %collective-permute-start.3 = (f32[64,66,1]{1,0,2:T(8,128)S(1)}, f32[64,66,1]{1,0,2:T(8,128)S(1)}, u32[]{:S(2)}, u32[]{:S(2)}) collective-permute-start(f32[64,66,1]{1,0,2:T(8,128)S(1)} %copy.134), channel_id=1, source_target_pairs={{4,0},{8,4},{12,8},{16,12},{20,16},{24,20},{28,24},{5,1},{9,5},{13... | collective-permute-start | bytes 50696 | tf_op jit(solution)/shard_map/ppermute | solution.py:25
  90.4 3.1 copy-start.17
  101.4 5.5 %copy-start.7 = (f32[16,4,64,128]{3,2,0,1:T(8,128)S(1)}, f32[16,4,64,128]{3,2,0,1:T(8,128)}, u32[]{:S(2)}) copy-start(f32[16,4,64,128]{3,2,0,1:T(8,128)} %copy.128) | copy-start | bytes 6291460
  101.4 5.5 %copy-start.12 = (f32[64,66,1]{2,1,0:T(8,128)S(1)}, f32[64,66,1]{2,1,0:T(8,128)}, u32[]{:S(2)}) copy-start(f32[64,66,1]{2,1,0:T(8,128)} %copy.135) | copy-start | bytes 50692
  101.4 5.5 %copy-start.15 = (f32[64,66,1]{2,1,0:T(8,128)S(1)}, f32[64,66,1]{2,1,0:T(8,128)}, u32[]{:S(2)}) copy-start(f32[64,66,1]{2,1,0:T(8,128)} %copy.136) | copy-start | bytes 50692
  106.8 7.1 %copy-start.22 = (u32[128]{0:T(128)S(1)}, u32[128]{0:T(128)}, u32[]{:S(2)}) copy-start(u32[128]{0:T(128)} %constant.47) | copy-start | bytes 1540
  106.9 20.3 %copy-start.21 = (u32[128]{0:T(128)S(1)}, u32[128]{0:T(128)}, u32[]{:S(2)}) copy-start(u32[128]{0:T(128)} %constant.52) | copy-start | bytes 1540
  106.9 36.3 %copy-start.20 = (u32[128]{0:T(128)S(1)}, u32[128]{0:T(128)}, u32[]{:S(2)}) copy-start(u32[128]{0:T(128)} %constant.57) | copy-start | bytes 1540
  106.9 46.2 %copy-start.19 = (u32[128]{0:T(128)S(1)}, u32[128]{0:T(128)}, u32[]{:S(2)}) copy-start(u32[128]{0:T(128)} %constant.62) | copy-start | bytes 1540
  177.0 63.1 %copy-start = (f32[64,64,128]{2,1,0:T(8,128)}, f32[64,64,128]{2,1,0:T(8,128)S(1)}, u32[]{:S(2)}) copy-start(f32[64,64,128]{2,1,0:T(8,128)S(1)} %bitcast_subtract_fusion) | copy-start | bytes 6291460
  205.3 8.2 %copy-start.3 = (f32[8,8,64,128]{3,2,1,0:T(8,128)}, f32[8,8,64,128]{3,2,1,0:T(8,128)S(1)}, u32[]{:S(2)}) copy-start(f32[8,8,64,128]{3,2,1,0:T(8,128)S(1)} %copy.170) | copy-start | bytes 6291460
  205.3 4.9 collective-permute-start.4
  208.3 5.2 %collective-permute-start.5 = (f32[64,1,128]{2,0,1:T(8,128)S(1)}, f32[64,1,128]{2,0,1:T(8,128)S(1)}, u32[]{:S(2)}, u32[]{:S(2)}) collective-permute-start(f32[64,1,128]{2,0,1:T(8,128)S(1)} %bitcast.300), channel_id=1, source_target_pairs={{1,0},{2,1},{3,2},{32,3},{33,32},{34,33},{35,34},{64,35},{65,64},{... | collective-permute-start | bytes 98312 | tf_op jit(solution)/shard_map/ppermute | solution.py:25
  219.2 7.5 %collective-permute-start.6 = (f32[64,66,1]{1,0,2:T(8,128)S(1)}, f32[64,66,1]{1,0,2:T(8,128)S(1)}, u32[]{:S(2)}, u32[]{:S(2)}) collective-permute-start(f32[64,66,1]{1,0,2:T(8,128)S(1)} %copy.145), channel_id=1, source_target_pairs={{0,4},{4,8},{8,12},{12,16},{16,20},{20,24},{24,28},{1,5},{5,9},{9,... | collective-permute-start | bytes 50696 | tf_op jit(solution)/shard_map/ppermute | solution.py:23
  225.4 6.2 %collective-permute-start.7 = (f32[64,66,1]{1,0,2:T(8,128)S(1)}, f32[64,66,1]{1,0,2:T(8,128)S(1)}, u32[]{:S(2)}, u32[]{:S(2)}) collective-permute-start(f32[64,66,1]{1,0,2:T(8,128)S(1)} %copy.146), channel_id=1, source_target_pairs={{4,0},{8,4},{12,8},{16,12},{20,16},{24,20},{28,24},{5,1},{9,5},{13... | collective-permute-start | bytes 50696 | tf_op jit(solution)/shard_map/ppermute | solution.py:25
  233.8 6.3 %copy-start.4 = (f32[8,8,64,128]{3,2,1,0:T(8,128)S(1)}, f32[8,8,64,128]{3,2,1,0:T(8,128)}, u32[]{:S(2)}) copy-start(f32[8,8,64,128]{3,2,1,0:T(8,128)} %copy-done.3) | copy-start | bytes 6291460
  233.8 6.3 %copy-start.8 = (f32[16,4,64,128]{3,2,0,1:T(8,128)S(1)}, f32[16,4,64,128]{3,2,0,1:T(8,128)}, u32[]{:S(2)}) copy-start(f32[16,4,64,128]{3,2,0,1:T(8,128)} %copy.128) | copy-start | bytes 6291460
  233.8 6.3 %copy-start.11 = (f32[64,66,1]{2,1,0:T(8,128)S(1)}, f32[64,66,1]{2,1,0:T(8,128)}, u32[]{:S(2)}) copy-start(f32[64,66,1]{2,1,0:T(8,128)} %copy.147) | copy-start | bytes 50692
  233.8 6.3 %copy-start.14 = (f32[64,66,1]{2,1,0:T(8,128)S(1)}, f32[64,66,1]{2,1,0:T(8,128)}, u32[]{:S(2)}) copy-start(f32[64,66,1]{2,1,0:T(8,128)} %copy.148) | copy-start | bytes 50692
  333.2 7.2 %copy-start.5 = (f32[8,8,64,128]{3,2,1,0:T(8,128)}, f32[8,8,64,128]{3,2,1,0:T(8,128)S(1)}, u32[]{:S(2)}) copy-start(f32[8,8,64,128]{3,2,1,0:T(8,128)S(1)} %copy.172) | copy-start | bytes 6291460
  333.2 4.3 collective-permute-start.8
  335.2 5.2 %collective-permute-start.9 = (f32[64,1,128]{2,0,1:T(8,128)S(1)}, f32[64,1,128]{2,0,1:T(8,128)S(1)}, u32[]{:S(2)}, u32[]{:S(2)}) collective-permute-start(f32[64,1,128]{2,0,1:T(8,128)S(1)} %bitcast.301), channel_id=1, source_target_pairs={{1,0},{2,1},{3,2},{32,3},{33,32},{34,33},{35,34},{64,35},{65,64},{... | collective-permute-start | bytes 98312 | tf_op jit(solution)/shard_map/ppermute | solution.py:25
  346.1 9.1 %collective-permute-start.10 = (f32[64,66,1]{1,0,2:T(8,128)S(1)}, f32[64,66,1]{1,0,2:T(8,128)S(1)}, u32[]{:S(2)}, u32[]{:S(2)}) collective-permute-start(f32[64,66,1]{1,0,2:T(8,128)S(1)} %copy.157), channel_id=1, source_target_pairs={{0,4},{4,8},{8,12},{12,16},{16,20},{20,24},{24,28},{1,5},{5,9},{9,... | collective-permute-start | bytes 50696 | tf_op jit(solution)/shard_map/ppermute | solution.py:23
  353.9 6.2 %collective-permute-start.11 = (f32[64,66,1]{1,0,2:T(8,128)S(1)}, f32[64,66,1]{1,0,2:T(8,128)S(1)}, u32[]{:S(2)}, u32[]{:S(2)}) collective-permute-start(f32[64,66,1]{1,0,2:T(8,128)S(1)} %copy.158), channel_id=1, source_target_pairs={{4,0},{8,4},{12,8},{16,12},{20,16},{24,20},{28,24},{5,1},{9,5},{13... | collective-permute-start | bytes 50696 | tf_op jit(solution)/shard_map/ppermute | solution.py:25
  362.3 6.3 %copy-start.6 = (f32[8,8,64,128]{3,2,1,0:T(8,128)S(1)}, f32[8,8,64,128]{3,2,1,0:T(8,128)}, u32[]{:S(2)}) copy-start(f32[8,8,64,128]{3,2,1,0:T(8,128)} %copy-done.5) | copy-start | bytes 6291460
  362.3 6.3 %copy-start.9 = (f32[16,4,64,128]{3,2,0,1:T(8,128)S(1)}, f32[16,4,64,128]{3,2,0,1:T(8,128)}, u32[]{:S(2)}) copy-start(f32[16,4,64,128]{3,2,0,1:T(8,128)} %copy.128) | copy-start | bytes 6291460
  362.3 6.3 %copy-start.10 = (f32[64,66,1]{2,1,0:T(8,128)S(1)}, f32[64,66,1]{2,1,0:T(8,128)}, u32[]{:S(2)}) copy-start(f32[64,66,1]{2,1,0:T(8,128)} %copy.159) | copy-start | bytes 50692
  362.3 6.3 %copy-start.13 = (f32[64,66,1]{2,1,0:T(8,128)S(1)}, f32[64,66,1]{2,1,0:T(8,128)}, u32[]{:S(2)}) copy-start(f32[64,66,1]{2,1,0:T(8,128)} %copy.160) | copy-start | bytes 50692
